TPU v7x, 32 devices: a whole 2x2x4 slice. The times are simulated.
32 devices in a mesh: seq: 8 (over z, x), expert: 4 (over y, core).
Axes of the slice: x: 2, y: 2, z: 4, core: 2. Of those that a mesh axis runs over, the one named last changes fastest.
Arguments:
- tokens: bfloat16 [1024, 4096], P('seq'), may hold values from -6 to 6
- norm_gain: float32 [4096], replicated, may hold values from 0.1 to 1.9
- router_weight: bfloat16 [4096, 4], replicated, may hold values from -0.09375 to 0.09375
- expert_ids: int32 [1024, 2], P('seq'), may hold values from 0 to 3, all different within a row; in each aligned block of 128 rows (0 to 127, 128 to 255, ...) at most 80 rows name the same one
- gate_weight: bfloat16 [4, 4096, 8192], P('expert', None, 'seq'), may hold values from -0.09375 to 0.09375
- up_weight: bfloat16 [4, 4096, 8192], P('expert', None, 'seq'), may hold values from -0.09375 to 0.09375
- down_weight: bfloat16 [4, 8192, 4096], P('expert', 'seq'), may hold values from -0.0625 to 0.0625
- query_weight: bfloat16 [4096, 2048], P(None, 'expert'), may hold values from -0.09375 to 0.09375
- key_weight: bfloat16 [4096, 2048], P(None, 'expert'), may hold values from -0.09375 to 0.09375
- log_decay: float32 [32, 1024], P('expert', 'seq'), may hold values from -1.5 to 0
- carried_state: float32 [32, 64, 128], P('expert'), may hold values from -48 to 48
- out_gain: float32 [4096], P('expert'), may hold values from 0.1 to 1.9
Outputs:
- teacher_out: bfloat16 [1024, 4096], P('seq', 'expert')
- student_out: bfloat16 [1024, 4096], P('seq', 'expert')
- token_loss: float32 [1024], P('seq')
Inputs may be any that keep to these rules, and one draw needn't show every extreme that they name: `expert_ids`: each token names 2 different experts. Among the 128 tokens of one block no expert is named by more than 80 tokens, and in every draw some expert is named by exactly 80 tokens of some block.
All inputs are finite; a program needn't handle non-finite values.
Results may differ from a plain program's by a relative error of at most 0.01.
Values may be sent and summed in bfloat16 or wider, within the bound.
A program may use at most 128 MiB of HBM per device.

v0:
```python
import functools
import jax
import jax.numpy as jnp
from jax import lax
from jax.experimental import pallas as pl
from jax.experimental.pallas import tpu as pltpu
from jax.sharding import PartitionSpec as P

norm_epsilon = 1e-05
head_epsilon = 1e-06
exact = lax.Precision.HIGHEST
f32 = jnp.float32
bf16 = jnp.bfloat16
LANES = 128
SUB = 8
MESH = pl.DeviceIdType.MESH


def ring_order(mesh):
    n = mesh.shape["seq"]
    line = mesh.devices[:, 0]
    coords = [getattr(d, "coords", None) for d in line]
    if any(c is None for c in coords):
        return list(range(n))
    places = {(c[0], c[2]): i for i, c in enumerate(coords)}
    xs = sorted({x for x, _ in places})
    zs = sorted({z for _, z in places})
    if len(places) != n or len(xs) * len(zs) != n or len(xs) % 2 or len(zs) < 2:
        return list(range(n))
    order = [places[(x, zs[0])] for x in xs]
    for turn, x in enumerate(reversed(xs)):
        column = zs[1:] if turn % 2 == 0 else zs[:0:-1]
        order += [places[(x, z)] for z in column]
    return order


def split(value):
    high = value.astype(bf16)
    low = (value - high.astype(f32)).astype(bf16)
    return high, low


def dot(a, b, dims=(1, 0), precision=None):
    return lax.dot_general(
        a,
        b,
        (((dims[0],), (dims[1],)), ((), ())),
        preferred_element_type=f32,
        precision=precision,
    )


def layer_kernel(
    order,
    cap,
    tok_hbm,
    gain,
    router,
    ids,
    gate_hbm,
    up_hbm,
    down_hbm,
    query_hbm,
    key_hbm,
    decay,
    carried,
    out_gain,
    teacher_out,
    student_out,
    loss_out,
    tok,
    gate,
    up,
    down,
    wq,
    wk,
    normed,
    rows,
    part,
    inbox,
    lhs,
    hid,
    qs,
    ks,
    run_s,
    run_t,
    retain_own,
    block_state,
    prior,
    pair_out,
    pair_in,
    retain_in,
    chain_out,
    chain_in,
    mix_high,
    mix_low,
    intra,
    expert_out,
    expert_in,
    loss_all,
    load_sem,
    ag_send,
    ag_recv,
    rs_send,
    rs_recv,
    st_send,
    st_recv,
    ex_send,
    ex_recv,
    lo_send,
    lo_recv,
):
    n = len(order)
    half = n // 2
    span, width = tok.shape
    half_cols = width // 2
    ff = gate.shape[1]
    groups = lax.axis_size("expert")
    bw = width // groups
    g = rows.shape[2]
    capp = g * SUB
    heads = decay.shape[0]
    key_size = block_state.shape[0] // heads
    per = LANES // key_size
    place = lax.axis_index("seq")
    mine = lax.axis_index("expert")
    pairs = n // 2
    pair = place // 2
    odd = place % 2

    def table(values):
        found = jnp.int32(0)
        for i, v in enumerate(values):
            found = jnp.where(place == i, jnp.int32(v), found)
        return found

    at = {s: k for k, s in enumerate(order)}
    right = table([order[(at[i] + 1) % n] for i in range(n)])
    left = table([order[(at[i] - 1) % n] for i in range(n)])
    sides = (right, left)
    partner = place + 1 - 2 * odd
    ahead = lax.rem(place + 2, n)
    behind = lax.rem(place + n - 2, n)

    loads = []
    for i, (src, dst) in enumerate(
        ((tok_hbm, tok), (key_hbm, wk), (query_hbm, wq), (gate_hbm, gate), (up_hbm, up), (down_hbm, down))
    ):
        copy = pltpu.make_async_copy(src, dst, load_sem.at[i])
        copy.start()
        loads.append(copy)

    barrier = pltpu.get_barrier_semaphore()
    for there in (right, left, partner, ahead, behind):
        pl.semaphore_signal(barrier, inc=1, device_id={"seq": there}, device_id_type=MESH)
    for shift in range(1, groups):
        peer = lax.rem(mine + shift, groups)
        pl.semaphore_signal(barrier, inc=1, device_id={"expert": peer}, device_id_type=MESH)

    sent = []

    def send(src, dst, send_sem, recv_sem, **to):
        copy = pltpu.make_async_remote_copy(
            src_ref=src,
            dst_ref=dst,
            send_sem=send_sem,
            recv_sem=recv_sem,
            device_id=to,
            device_id_type=MESH,
        )
        copy.start()
        return copy

    def arrived(dst, sem):
        pltpu.make_async_copy(dst, dst, sem).wait()

    loads[0].wait()
    strip = 16

    def norm_strip(i, _):
        at_rows = pl.ds(pl.multiple_of(i * strip, strip), strip)
        x = tok[at_rows, :].astype(f32)
        scale = lax.rsqrt(jnp.mean(x * x, axis=1, keepdims=True) + norm_epsilon)
        normed[at_rows, :] = (x * scale * gain[...]).astype(bf16)
        return 0

    lax.fori_loop(0, span // strip, norm_strip, 0)
    experts = router.shape[1]
    logits = dot(normed[...], router[...])
    id0 = ids[:, 0:1]
    id1 = ids[:, 1:2]
    lane_e = lax.broadcasted_iota(jnp.int32, (span, experts), 1)
    chosen0 = jnp.sum(jnp.where(lane_e == id0, logits, 0.0), axis=1, keepdims=True)
    chosen1 = jnp.sum(jnp.where(lane_e == id1, logits, 0.0), axis=1, keepdims=True)
    share0 = 1.0 / (1.0 + jnp.exp(chosen1 - chosen0))
    share1 = 1.0 - share0
    row_t = lax.broadcasted_iota(jnp.int32, (span, span), 0)
    col_t = lax.broadcasted_iota(jnp.int32, (span, span), 1)
    lane = lax.broadcasted_iota(jnp.int32, (span, LANES), 1)
    hits = jnp.where((lane == id0) | (lane == id1), 1.0, 0.0).astype(bf16)
    before = jnp.where(row_t > col_t, 1.0, 0.0).astype(bf16)
    slots = dot(before, hits)
    own_lane = jnp.where(
        lax.broadcasted_iota(jnp.int32, (SUB, LANES), 1) == mine, 1.0, 0.0
    ).astype(bf16)
    hit_row = dot(own_lane, hits, (1, 1))
    slot_row = dot(own_lane, slots.astype(bf16), (1, 1))
    want = lax.broadcasted_iota(jnp.int32, (capp, span), 0)
    picked = (slot_row[0:1, :].astype(jnp.int32) == want) & (hit_row[0:1, :] > 0.5) & (want < cap)
    select = jnp.where(picked, 1.0, 0.0).astype(bf16)
    step_cols = 512
    for h in range(2):

        def dispatch(i, _, h=h):
            off = pl.multiple_of(i * step_cols, step_cols)
            got = dot(select, normed[:, pl.ds(h * half_cols + off, step_cols)])
            rows[0, h, :, :, pl.ds(off, step_cols)] = got.reshape(g, SUB, step_cols).astype(bf16)
            return 0

        lax.fori_loop(0, half_cols // step_cols, dispatch, 0)

    pl.semaphore_wait(barrier, 5 + groups - 1)

    def spot(rel):
        return rel % n

    def ag_step(k, side, h):
        sign = -1 if side == 0 else 1
        src = spot(sign * (k - 1))
        dst = spot(sign * k)
        sent.append(
            send(
                rows.at[src, h],
                rows.at[dst, h],
                ag_send.at[side, k, h],
                ag_recv.at[side, k, h],
                seq=sides[side],
            )
        )

    for ci in range(2):
        for side in range(2):
            ag_step(1, side, ci if side == 0 else 1 - ci)

    def ag_event(k, ci):
        for side in range(2):
            h = ci if side == 0 else 1 - ci
            sign = -1 if side == 0 else 1
            arrived(rows.at[spot(sign * k), h], ag_recv.at[side, k, h])
            if k + 1 < half or (k + 1 == half and ci == 0):
                ag_step(k + 1, side, h)

    wide = groups * capp
    lane_w = lax.broadcasted_iota(jnp.int32, (span, wide), 1)
    mixing = jnp.zeros((span, wide), f32)
    for shift in range(groups):
        source = lax.rem(mine + groups - shift, groups)
        slot = jnp.sum(jnp.where(lane == source, slots, 0.0), axis=1, keepdims=True).astype(jnp.int32)
        first, second = id0 == source, id1 == source
        share = jnp.where(first, share0, jnp.where(second, share1, 0.0))
        share = jnp.where(slot < cap, share, 0.0)
        mixing = mixing + jnp.where(lane_w == slot + shift * capp, share, 0.0)
    high, low = split(mixing)
    mix_high[...] = high
    mix_low[...] = low

    loads[1].wait()
    ks[...] = dot(tok[...], wk[...])
    loads[2].wait()
    qs[...] = dot(tok[...], wq[...])

    lower = row_t >= col_t
    tri = jnp.where(lower, 1.0, 0.0)
    run_s[...] = dot(decay[...], tri, (1, 1), exact)
    run_t[...] = dot(tri, decay[...], (1, 1), exact)
    retain_own[...] = jnp.exp(jnp.broadcast_to(run_s[:, span - 1 : span], (heads, LANES)))

    def values_of(head):
        return tok[:, pl.ds(pl.multiple_of(mine * bw + head * LANES, LANES), LANES)]

    def state_unit(p):
        tail = jnp.exp(run_t[span - 1 : span, :] - run_t[...])
        factor = jnp.zeros((span, LANES), f32)
        for a in range(per):
            inside = (lane >= a * key_size) & (lane < (a + 1) * key_size)
            factor = jnp.where(inside, tail[:, p * per + a : p * per + a + 1], factor)
        scaled = (ks[:, p * LANES : (p + 1) * LANES] * factor).T
        hi, lo = split(scaled)
        for a in range(per):
            head = p * per + a
            values = values_of(head)
            cut = slice(a * key_size, (a + 1) * key_size)
            block_state[head * key_size : (head + 1) * key_size, :] = (
                dot(hi, values) + dot(lo, values)
            )[cut]

    for p in range(heads // per):
        state_unit(p)
    pair_out[...] = block_state[...].astype(bf16)
    state_sent = [
        send(pair_out, pair_in, st_send.at[0], st_recv.at[0], seq=partner),
        send(retain_own, retain_in, st_send.at[1], st_recv.at[1], seq=partner),
    ]

    def chain_point(j):
        if j == 0:
            arrived(pair_in, st_recv.at[0])
            arrived(retain_in, st_recv.at[1])

        @pl.when(pair == j)
        def _():
            if j > 0:
                arrived(chain_in, st_recv.at[2])
            for head in range(heads):
                at_head = slice(head * key_size, (head + 1) * key_size)
                coming = carried[at_head, :] if j == 0 else chain_in[at_head, :].astype(f32)
                own_keep = retain_own[head : head + 1, :]
                other_keep = retain_in[head : head + 1, :]
                own = block_state[at_head, :]
                other = pair_in[at_head, :].astype(f32)
                is_odd = odd == 1
                prior[at_head, :] = jnp.where(is_odd, other_keep * coming + other, coming)
                if j < pairs - 1:
                    both = jnp.where(is_odd, own_keep * other + own, other_keep * own + other)
                    chain_out[at_head, :] = (own_keep * other_keep * coming + both).astype(bf16)
            if j < pairs - 1:
                send(chain_out, chain_in, st_send.at[2], st_recv.at[2], seq=ahead)

    batches = [[0]] + [[k, -k] for k in range(1, half)] + [[half]]

    def gate_up(b):
        members = batches[b]
        m = len(members) * capp

        def gather(i, _):
            off = pl.multiple_of(i * step_cols, step_cols)
            for h in range(2):
                got = [
                    rows[spot(rel), h, :, :, pl.ds(off, step_cols)].astype(f32).reshape(capp, step_cols)
                    for rel in members
                ]
                got = jnp.concatenate(got, axis=0) if len(got) > 1 else got[0]
                lhs[0:m, pl.ds(h * half_cols + off, step_cols)] = got.astype(bf16)
            return 0

        lax.fori_loop(0, half_cols // step_cols, gather, 0)
        tile = min(256, ff)

        def columns(i, _):
            cols = pl.ds(pl.multiple_of(i * tile, tile), tile)
            a = lhs[0:m, :]
            gated = dot(a, gate[:, cols])
            upped = dot(a, up[:, cols])
            silu = gated / (1.0 + jnp.exp(-gated))
            hid[b, 0:m, cols] = (silu * upped).astype(bf16)
            return 0

        lax.fori_loop(0, ff // tile, columns, 0)

    def down_proj(b, h):
        members = batches[b]
        m = len(members) * capp

        def columns(i, _):
            off = pl.multiple_of(i * step_cols, step_cols)
            got = dot(hid[b, 0:m, :], down[:, pl.ds(h * half_cols + off, step_cols)])
            for j, rel in enumerate(members):
                piece = got[j * capp : (j + 1) * capp].reshape(g, SUB, step_cols)
                part[spot(rel), h, :, :, pl.ds(off, step_cols)] = piece.astype(bf16)
            return 0

        lax.fori_loop(0, half_cols // step_cols, columns, 0)

    def rs_step(k, side, h, add):
        rel = spot(k if side == 0 else -k)
        if add:
            arrived(inbox.at[side, k + 1, h], rs_recv.at[side, k + 1, h])

            def add_cols(i, _):
                cols = pl.ds(pl.multiple_of(i * step_cols, step_cols), step_cols)
                total = part[rel, h, :, :, cols].astype(f32) + inbox[side, k + 1, h, :, :, cols].astype(f32)
                part[rel, h, :, :, cols] = total.astype(bf16)
                return 0

            lax.fori_loop(0, half_cols // step_cols, add_cols, 0)
        sent.append(
            send(
                part.at[rel, h],
                inbox.at[side, k, h],
                rs_send.at[side, k, h],
                rs_recv.at[side, k, h],
                seq=sides[side],
            )
        )

    def free_chain(k, add):
        for side in range(2):
            rs_step(k, side, 1 - side, add)

    def far_chain(k, add):
        for side in range(2):
            rs_step(k, side, side, add)

    def intra_unit(p):
        q_pair = qs[:, p * LANES : (p + 1) * LANES]
        k_hi, k_lo = split(ks[:, p * LANES : (p + 1) * LANES])
        for a in range(per):
            head = p * per + a
            inside = (lane >= a * key_size) & (lane < (a + 1) * key_size)
            q_hi, q_lo = split(jnp.where(inside, q_pair, 0.0))
            scores = dot(q_hi, k_hi, (1, 1)) + dot(q_hi, k_lo, (1, 1)) + dot(q_lo, k_hi, (1, 1))
            gaps = run_t[:, head : head + 1] - run_s[head : head + 1, :]
            scores = scores * jnp.where(row_t >= col_t, jnp.exp(jnp.minimum(gaps, 0.0)), 0.0)
            s_hi, s_lo = split(scores)
            values = values_of(head)
            intra[:, head * LANES : (head + 1) * LANES] = dot(s_hi, values) + dot(s_lo, values)

    def inter_unit(p):
        q_pair = qs[:, p * LANES : (p + 1) * LANES]
        s_hi, s_lo = split(prior[p * LANES : (p + 1) * LANES, :])
        for a in range(per):
            head = p * per + a
            cols = slice(head * LANES, (head + 1) * LANES)
            inside = (lane >= a * key_size) & (lane < (a + 1) * key_size)
            q_hi, q_lo = split(jnp.where(inside, q_pair, 0.0))
            carried_rows = dot(q_hi, s_hi) + dot(q_hi, s_lo) + dot(q_lo, s_hi)
            out = intra[:, cols] + jnp.exp(run_t[:, head : head + 1]) * carried_rows
            scale = lax.rsqrt(jnp.mean(out * out, axis=1, keepdims=True) + head_epsilon)
            hidden = values_of(head).astype(f32) + out * scale * out_gain[:, cols]
            intra[:, cols] = hidden
            student_out[:, cols] = hidden.astype(bf16)

    loads[3].wait()
    loads[4].wait()
    for k in range(1, half):
        ag_event(k, 0)
        if k == 1:
            gate_up(0)
        if k == 2:
            chain_point(0)
            for p in range(heads // per):
                intra_unit(p)
        ag_event(k, 1)
        gate_up(k)
    loads[5].wait()
    down_proj(half - 1, 0)
    down_proj(half - 1, 1)
    free_chain(half - 1, False)
    ag_event(half, 0)
    gate_up(half)
    down_proj(half, 0)
    down_proj(half, 1)
    far_chain(half, False)
    link = 1
    for k in range(half - 1, 0, -1):
        if link < pairs:
            chain_point(link)
            link += 1
        for h in range(2):
            down_proj(k - 1, h)
        if k > 1:
            free_chain(k - 1, True)
        else:
            for p in range(heads // per):
                inter_unit(p)
        far_chain(k, True)

    for side in range(2):
        for h in range(2):
            arrived(inbox.at[side, 1, h], rs_recv.at[side, 1, h])
    per_half = groups // 2
    for q in range(groups):
        h = q // per_half
        cols = pl.ds((q % per_half) * bw, bw)
        total = part[0, h, :, :, cols].astype(f32)
        total = total + inbox[0, 1, h, :, :, cols].astype(f32) + inbox[1, 1, h, :, :, cols].astype(f32)
        expert_out[q] = total.astype(bf16)
    for shift in [groups // 2] + [i for i in range(1, groups) if i != groups // 2]:
        peer = lax.rem(mine + shift, groups)
        sent.append(
            send(
                expert_out.at[peer], expert_in.at[shift], ex_send.at[shift], ex_recv.at[shift], expert=peer
            )
        )
    expert_in[0] = expert_out[mine]
    for shift in range(1, groups):
        arrived(expert_in.at[shift], ex_recv.at[shift])
    loss_row = jnp.zeros((SUB, span), f32)
    ones = jnp.ones((SUB, step_cols), f32)
    for i in range(bw // step_cols):
        cols = slice(i * step_cols, (i + 1) * step_cols)
        got = [expert_in[shift, :, :, cols].astype(f32).reshape(capp, step_cols) for shift in range(groups)]
        got = jnp.concatenate(got, axis=0).astype(bf16)
        mixed = dot(mix_high[...], got) + dot(mix_low[...], got)
        own = tok[:, pl.ds(pl.multiple_of(mine * bw + i * step_cols, LANES), step_cols)].astype(f32)
        hidden = own + mixed
        teacher_out[:, cols] = hidden.astype(bf16)
        gap = intra[:, cols] - hidden
        loss_row = loss_row + dot(ones, gap * gap, (1, 1), exact)
    loss_all[mine] = loss_row
    for shift in range(1, groups):
        peer = lax.rem(mine + shift, groups)
        sent.append(
            send(loss_all.at[mine], loss_all.at[mine], lo_send.at[shift], lo_recv.at[mine], expert=peer)
        )
    for shift in range(1, groups):
        peer = lax.rem(mine + shift, groups)
        arrived(loss_all.at[peer], lo_recv.at[peer])
    total = loss_all[0]
    for q in range(1, groups):
        total = total + loss_all[q]
    loss_out[...] = total / width

    for copy in sent + state_sent:
        copy.wait_send()

    @pl.when(pair < pairs - 1)
    def _():
        pltpu.make_async_copy(chain_out, chain_out, st_send.at[2]).wait()


def on_device(
    order,
    tokens,
    norm_gain,
    router_weight,
    expert_ids,
    gate_weight,
    up_weight,
    down_weight,
    query_weight,
    key_weight,
    log_decay,
    carried_state,
    out_gain,
):
    span, width = tokens.shape
    experts = router_weight.shape[1]
    groups = lax.axis_size("expert")
    cap = 7 * expert_ids.shape[1] * span // (8 * experts)
    g = -(-cap // SUB)
    capp = g * SUB
    n = len(order)
    half = n // 2
    half_cols = width // 2
    ff = gate_weight.shape[2]
    bw = width // groups
    heads, key_size, feats = carried_state.shape
    keys = heads * key_size
    hbm = pl.BlockSpec(memory_space=pl.ANY)
    vmem = pl.BlockSpec(memory_space=pltpu.VMEM)
    dma = pltpu.SemaphoreType.DMA
    scratch = [
        pltpu.VMEM((span, width), bf16),
        pltpu.VMEM((width, ff), bf16),
        pltpu.VMEM((width, ff), bf16),
        pltpu.VMEM((ff, width), bf16),
        pltpu.VMEM((width, keys), bf16),
        pltpu.VMEM((width, keys), bf16),
        pltpu.VMEM((span, width), bf16),
        pltpu.VMEM((n, 2, g, SUB, half_cols), bf16),
        pltpu.VMEM((n, 2, g, SUB, half_cols), bf16),
        pltpu.VMEM((2, half + 1, 2, g, SUB, half_cols), bf16),
        pltpu.VMEM((2 * capp, width), bf16),
        pltpu.VMEM((half + 1, 2 * capp, ff), bf16),
        pltpu.VMEM((span, keys), f32),
        pltpu.VMEM((span, keys), f32),
        pltpu.VMEM((heads, span), f32),
        pltpu.VMEM((span, heads), f32),
        pltpu.VMEM((heads, LANES), f32),
        pltpu.VMEM((keys, feats), f32),
        pltpu.VMEM((keys, feats), f32),
        pltpu.VMEM((keys, feats), bf16),
        pltpu.VMEM((keys, feats), bf16),
        pltpu.VMEM((heads, LANES), f32),
        pltpu.VMEM((keys, feats), bf16),
        pltpu.VMEM((keys, feats), bf16),
        pltpu.VMEM((span, groups * capp), bf16),
        pltpu.VMEM((span, groups * capp), bf16),
        pltpu.VMEM((span, bw), f32),
        pltpu.VMEM((groups, g, SUB, bw), bf16),
        pltpu.VMEM((groups, g, SUB, bw), bf16),
        pltpu.VMEM((groups, SUB, span), f32),
        dma((6,)),
        dma((2, half + 1, 2)),
        dma((2, half + 1, 2)),
        dma((2, half + 1, 2)),
        dma((2, half + 1, 2)),
        dma((3,)),
        dma((3,)),
        dma((groups,)),
        dma((groups,)),
        dma((groups,)),
        dma((groups,)),
    ]
    teacher, student, loss = pl.pallas_call(
        functools.partial(layer_kernel, order, cap),
        out_shape=(
            jax.ShapeDtypeStruct((span, bw), bf16),
            jax.ShapeDtypeStruct((span, bw), bf16),
            jax.ShapeDtypeStruct((SUB, span), f32),
        ),
        in_specs=[hbm, vmem, vmem, vmem, hbm, hbm, hbm, hbm, hbm, vmem, vmem, vmem],
        out_specs=(vmem, vmem, vmem),
        scratch_shapes=scratch,
        compiler_params=pltpu.CompilerParams(
            collective_id=0, has_side_effects=True, vmem_limit_bytes=62 * 1024 * 1024
        ),
        name="layer",
    )(
        tokens,
        norm_gain.reshape(1, width),
        router_weight,
        expert_ids,
        gate_weight.reshape(width, ff),
        up_weight.reshape(width, ff),
        down_weight.reshape(ff, width),
        query_weight,
        key_weight,
        log_decay,
        carried_state.reshape(keys, feats),
        out_gain.reshape(1, bw),
    )
    return teacher, student, loss[0]


def solution(mesh):
    return jax.shard_map(
        functools.partial(on_device, tuple(ring_order(mesh))),
        mesh=mesh,
        in_specs=(
            P("seq", None),
            P(),
            P(),
            P("seq", None),
            P("expert", None, "seq"),
            P("expert", None, "seq"),
            P("expert", "seq", None),
            P(None, "expert"),
            P(None, "expert"),
            P("expert", "seq"),
            P("expert", None, None),
            P("expert"),
        ),
        out_specs=(P("seq", "expert"), P("seq", "expert"), P("seq")),
        check_vma=False,
    )
```

profile of v0, /device:TPU:0, one launch (start us, length us, event | category | flops | bytes accessed | tf_op | source)
XLA Modules:
  0.0 105.4 jit_solution(6594739374999551892)
XLA Ops:
  0.6 1.4 %copy.16.ids = s32[128,2]{1,0:T(8,128)} copy(s32[128,2]{0,1:T(2,128)} %param.15) | data formatting | bytes 2048 | tf_op args[3]
  2.0 2.2 %copy.15.router = bf16[4096,4]{1,0:T(8,128)(2,1)} copy(bf16[4096,4]{0,1:T(4,128)(2,1)} %param.14) | data formatting | bytes 65536 | tf_op args[2]
  4.2 96.6 %layer.1 = (bf16[128,1024]{1,0:T(8,128)(2,1)}, bf16[128,1024]{1,0:T(8,128)(2,1)}, f32[8,128]{1,0:T(8,128)}) custom-call(bf16[128,4096]{1,0:T(8,128)(2,1)} %tok_hbm.1, f32[1,4096]{1,0:T(1,128)} %bitcast.12, bf16[4096,4]{1,0:T(8,128)(2,1)} %copy.15.router, s32[128,2]{1,0:T(8,128)} %copy.16.ids, bf16[4096,1024]{1,0:T(8,128)(2,1)} %bitcast.8, ...), custom_call_target="tpu_custom_call" | custom-call | tf_op jit(solution)/shard_map/layer/pallas_call | solution.py:596
  100.8 1.2 %slice_bitcast_fusion = f32[128]{0:T(128)} fusion(f32[8,128]{1,0:T(8,128)} %get-tuple-element.8), kind=kLoop, calls=%fused_computation | loop fusion | bytes 1024 | tf_op jit(solution)/shard_map/squeeze | solution.py:624
  102.0 1.7 %copy.19 = bf16[128,1024]{1,0:T(8,128)(2,1)} copy(bf16[128,1024]{1,0:T(8,128)(2,1)} %get-tuple-element.12) | data formatting | bytes 524288
  103.7 1.7 %copy.20 = bf16[128,1024]{1,0:T(8,128)(2,1)} copy(bf16[128,1024]{1,0:T(8,128)(2,1)} %get-tuple-element.13) | data formatting | bytes 524288
where the time goes:
time: 106 us; the launch traced here: 105 us
  Pallas kernels  96.6 us (91%)
  local copies, waits for them, and re-layouts  8.11 us (8%)
    pallas_call x1, Pallas kernels, on_device(): pl.pallas_call(functools.partial(layer_kernel, order, cap), out_shape=(ja...  96.6 us
    unnamed x4, local copies, waits for them, and re-layouts  6.91 us

commit v1 on v0

v1 whole, which is shorter than its diff:
```python
import functools
import jax
import jax.numpy as jnp
from jax import lax
from jax.experimental import pallas as pl
from jax.experimental.pallas import tpu as pltpu
from jax.sharding import PartitionSpec as P

norm_epsilon = 1e-05
head_epsilon = 1e-06
exact = lax.Precision.HIGHEST
f32 = jnp.float32
bf16 = jnp.bfloat16
LANES = 128
SUB = 8
MESH = pl.DeviceIdType.MESH


def ring_order(mesh):
    n = mesh.shape["seq"]
    line = mesh.devices[:, 0]
    coords = [getattr(d, "coords", None) for d in line]
    if any(c is None for c in coords):
        return list(range(n))
    places = {(c[0], c[2]): i for i, c in enumerate(coords)}
    xs = sorted({x for x, _ in places})
    zs = sorted({z for _, z in places})
    if len(places) != n or len(xs) * len(zs) != n or len(xs) % 2 or len(zs) < 2:
        return list(range(n))
    order = [places[(x, zs[0])] for x in xs]
    for turn, x in enumerate(reversed(xs)):
        column = zs[1:] if turn % 2 == 0 else zs[:0:-1]
        order += [places[(x, z)] for z in column]
    return order


def split(value):
    high = value.astype(bf16)
    low = (value - high.astype(f32)).astype(bf16)
    return high, low


def dot(a, b, dims=(1, 0), precision=None):
    return lax.dot_general(
        a,
        b,
        (((dims[0],), (dims[1],)), ((), ())),
        preferred_element_type=f32,
        precision=precision,
    )


class Plan:
    link_rate = 45000.0
    latency = 2.8

    def __init__(self):
        self.now = 0.0
        self.free = 0.0
        self.arrival = {}
        self.units = []
        self.done = set()

    def unit(self, name, cost, work, after=(), messages=(), start=0.0):
        self.units.append((name, cost, work, tuple(after), tuple(messages), start))

    def ready(self, unit):
        name, cost, work, after, messages, start = unit
        if any(a not in self.done for a in after) or any(m not in self.arrival for m in messages):
            return None
        return max([start] + [self.arrival[m] + 1.0 for m in messages])

    def run(self, unit):
        name, cost, work, after, messages, start = unit
        self.units.remove(unit)
        for a in after:
            self.force(a)
        self.now = max([self.now] + [self.arrival[m] for m in messages])
        work()
        self.now += cost
        self.done.add(name)

    def force(self, name):
        for unit in self.units:
            if unit[0] == name:
                self.run(unit)
                return
        assert name in self.done

    def fill(self, until):
        while True:
            for unit in self.units:
                when = self.ready(unit)
                if when is not None and when <= self.now and self.now + unit[1] <= until:
                    self.run(unit)
                    break
            else:
                later = [self.ready(u) for u in self.units]
                later = [w for w in later if w is not None and self.now < w < until]
                if not later:
                    return
                self.now = min(later)

    def message(self, name, size, work, before=None, needs=()):
        for a in needs:
            self.force(a)
        ready = self.arrival[before] if before is not None else self.now
        self.fill(max(ready, self.free - 0.5))
        self.now = max(self.now, ready)
        work()
        self.now += 0.1
        self.free = max(self.free, self.now) + size / self.link_rate
        self.arrival[name] = self.free + self.latency

    def drain(self):
        while self.units:
            known = [(self.ready(u), i) for i, u in enumerate(self.units)]
            known = [w for w in known if w[0] is not None]
            self.run(self.units[min(known)[1]])


def layer_kernel(
    order,
    cap,
    parts,
    cuts,
    tok_hbm,
    gain_hbm,
    router_hbm,
    ids_hbm,
    gate_hbm,
    up_hbm,
    down_hbm,
    query_hbm,
    key_hbm,
    decay_hbm,
    carried_hbm,
    out_gain_hbm,
    teacher_hbm,
    student_hbm,
    loss_out,
    gain,
    router,
    ids,
    decay,
    carried,
    out_gain,
    teacher_out,
    student_out,
    tok,
    gate,
    up,
    down,
    wq,
    wk,
    normed,
    lhs,
    qs,
    ks,
    run_s,
    run_t,
    retain_own,
    block_state,
    prior,
    pair_out,
    pair_in,
    retain_in,
    chain_out,
    chain_in,
    intra,
    teacher,
    slot_s,
    loss_all,
    rows,
    part,
    inbox,
    hid,
    mix_high,
    mix_low,
    expert_out,
    expert_in,
    load_sem,
    ag_send,
    ag_recv,
    rs_send,
    rs_recv,
    st_send,
    st_recv,
    ex_send,
    ex_recv,
    lo_send,
    lo_recv,
):
    n = len(order)
    half = n // 2
    span, width = tok.shape
    cut_cols = width // cuts
    ff = gate.shape[1]
    groups = lax.axis_size("expert")
    bw = width // groups
    capp = sum(parts) * SUB
    heads = decay.shape[0]
    key_size = block_state.shape[0] // heads
    per = LANES // key_size
    place = lax.axis_index("seq")
    mine = lax.axis_index("expert")
    pairs = n // 2
    pair = place // 2
    odd = place % 2
    step_cols = 512
    splits = range(len(parts))
    size_of = [p * SUB for p in parts]
    first_of = [sum(size_of[:t]) for t in splits]

    def table(values):
        found = jnp.int32(0)
        for i, v in enumerate(values):
            found = jnp.where(place == i, jnp.int32(v), found)
        return found

    at = {s: k for k, s in enumerate(order)}
    right = table([order[(at[i] + 1) % n] for i in range(n)])
    left = table([order[(at[i] - 1) % n] for i in range(n)])
    sides = (right, left)
    partner = place + 1 - 2 * odd
    ahead = lax.rem(place + 2, n)
    behind = lax.rem(place + n - 2, n)

    loads = [
        pltpu.make_async_copy(src, dst, load_sem.at[i])
        for i, (src, dst) in enumerate(
            (
                (tok_hbm, tok),
                (key_hbm, wk),
                (query_hbm, wq),
                (gate_hbm, gate),
                (up_hbm, up),
                (down_hbm, down),
                (ids_hbm, ids),
                (gain_hbm, gain),
                (decay_hbm, decay),
                (router_hbm, router),
                (carried_hbm, carried),
                (out_gain_hbm, out_gain),
            )
        )
    ]
    small = 6
    loads[small].start()
    loads[0].start()
    for copy in loads[small + 1 :]:
        copy.start()

    barrier = pltpu.get_barrier_semaphore()
    for there in (right, left, partner, ahead, behind):
        pl.semaphore_signal(barrier, inc=1, device_id={"seq": there}, device_id_type=MESH)
    for shift in range(1, groups):
        peer = lax.rem(mine + shift, groups)
        pl.semaphore_signal(barrier, inc=1, device_id={"expert": peer}, device_id_type=MESH)

    def send(src, dst, send_sem, recv_sem, **to):
        copy = pltpu.make_async_remote_copy(
            src_ref=src,
            dst_ref=dst,
            send_sem=send_sem,
            recv_sem=recv_sem,
            device_id=to,
            device_id_type=MESH,
        )
        copy.start()
        return copy

    def arrived(dst, sem):
        pltpu.make_async_copy(dst, dst, sem).wait()

    loads[small].wait()
    row_t = lax.broadcasted_iota(jnp.int32, (span, span), 0)
    col_t = lax.broadcasted_iota(jnp.int32, (span, span), 1)
    lane = lax.broadcasted_iota(jnp.int32, (span, LANES), 1)
    eye = jnp.where(row_t == col_t, 1.0, 0.0).astype(bf16)
    id_cols = dot(eye, ids[...].astype(f32).astype(bf16), (1, 1)).astype(jnp.int32)
    id0 = id_cols[:, 0:1]
    id1 = id_cols[:, 1:2]
    hits = jnp.where((lane == id0) | (lane == id1), 1.0, 0.0).astype(bf16)
    before = jnp.where(row_t > col_t, 1.0, 0.0).astype(bf16)
    slots = dot(before, hits)
    slot_s[...] = slots
    own_hit = jnp.where((ids[0:1, :] == mine) | (ids[1:2, :] == mine), 1.0, 0.0)
    own_hit = jnp.broadcast_to(own_hit, (SUB, span))
    own_slot = dot(own_hit.astype(bf16), before, (1, 1))
    want = lax.broadcasted_iota(jnp.int32, (capp, span), 0)
    picked = (own_slot[0:1, :].astype(jnp.int32) == want) & (own_hit[0:1, :] > 0.5) & (want < cap)
    select = jnp.where(picked, 1.0, 0.0).astype(bf16)

    loads[0].wait()
    loads[1].start()
    loads[2].start()
    loads[small + 1].wait()
    strip = 16

    def norm_strip(i, _):
        at_rows = pl.ds(pl.multiple_of(i * strip, strip), strip)
        x = tok[at_rows, :].astype(f32)
        scale = lax.rsqrt(jnp.mean(x * x, axis=1, keepdims=True) + norm_epsilon)
        normed[at_rows, :] = (x * scale * gain[...]).astype(bf16)
        return 0

    lax.fori_loop(0, span // strip, norm_strip, 0, unroll=4)
    loads[3].start()
    loads[4].start()
    for copy in loads[small + 2 :]:
        copy.wait()
    pl.semaphore_wait(barrier, 5 + groups - 1)
    ready_cuts = set()

    def dispatch(h):
        ready_cuts.add(h)
        for i in range(cut_cols // step_cols):
            off = i * step_cols
            got = dot(select, normed[:, h * cut_cols + off : h * cut_cols + off + step_cols])
            for t in splits:
                piece = got[first_of[t] : first_of[t] + size_of[t]].reshape(parts[t], SUB, step_cols)
                rows[t][0, h, :, :, off : off + step_cols] = piece.astype(bf16)

    plan = Plan()
    waited = set()

    def spot(rel):
        return rel % n

    def column_cut(message, side):
        kind, t, k, which = message
        return which if side == 0 else cuts - 1 - which

    def sem_of(message):
        kind, t, k, which = message
        return (ag_recv if kind == "ag" else rs_recv).at[t, (k - 1) * cuts + which]

    def need(message):
        if message in waited:
            return
        waited.add(message)
        both = inbox[message[1]].at[:, 0, 0]
        arrived(both, sem_of(message))

    def go(message):
        kind, t, k, which = message
        prev = (kind, t, k - 1 if kind == "ag" else k + 1, which)
        chained = prev in plan.arrival
        if chained:
            need(prev)
        for side in range(2):
            h = column_cut(message, side)
            if kind == "ag" and h not in ready_cuts:
                dispatch(h)
        for side in range(2):
            h = column_cut(message, side)
            if kind == "ag":
                sign = -1 if side == 0 else 1
                src = rows[t].at[spot(sign * (k - 1)), h]
                dst = rows[t].at[spot(sign * k), h]
                out = ag_send.at[t]
            else:
                rel = spot(k if side == 0 else -k)
                if chained:

                    def add_cols(i, _, side=side, h=h, rel=rel):
                        cols = pl.ds(pl.multiple_of(i * step_cols, step_cols), step_cols)
                        total = part[t][rel, h, :, :, cols].astype(f32)
                        total = total + inbox[t][side, k + 1, h, :, :, cols].astype(f32)
                        part[t][rel, h, :, :, cols] = total.astype(bf16)
                        return 0

                    lax.fori_loop(0, cut_cols // step_cols, add_cols, 0)
                src = part[t].at[rel, h]
                dst = inbox[t].at[side, k, h]
                out = rs_send.at[t]
            send(src, dst, out, sem_of(message), seq=sides[side])

    def mixing_unit():
        experts = router.shape[0]
        logits = dot(normed[...], router[...], (1, 1))
        lane_e = lax.broadcasted_iota(jnp.int32, (span, experts), 1)
        chosen0 = jnp.sum(jnp.where(lane_e == id0, logits, 0.0), axis=1, keepdims=True)
        chosen1 = jnp.sum(jnp.where(lane_e == id1, logits, 0.0), axis=1, keepdims=True)
        share0 = 1.0 / (1.0 + jnp.exp(chosen1 - chosen0))
        share1 = 1.0 - share0
        mixing = [jnp.zeros((span, groups * size), f32) for size in size_of]
        for shift in range(groups):
            source = lax.rem(mine + groups - shift, groups)
            slot = jnp.sum(jnp.where(lane == source, slot_s[...], 0.0), axis=1, keepdims=True).astype(jnp.int32)
            share = jnp.where(id0 == source, share0, jnp.where(id1 == source, share1, 0.0))
            for t in splits:
                inside = (slot >= first_of[t]) & (slot < min(first_of[t] + size_of[t], cap))
                lane_w = lax.broadcasted_iota(jnp.int32, mixing[t].shape, 1)
                here = lane_w == slot - first_of[t] + shift * size_of[t]
                mixing[t] = mixing[t] + jnp.where(here, jnp.where(inside, share, 0.0), 0.0)
        for t in splits:
            high, low = split(mixing[t])
            mix_high[t][...] = high
            mix_low[t][...] = low

    def keys_unit():
        loads[1].wait()
        ks[...] = dot(tok[...], wk[...])

    def queries_unit():
        loads[2].wait()
        qs[...] = dot(tok[...], wq[...])

    def decay_unit():
        tri = jnp.where(row_t >= col_t, 1.0, 0.0)
        run_s[...] = dot(decay[...], tri, (1, 1), exact)
        run_t[...] = dot(tri, decay[...], (1, 1), exact)
        retain_own[...] = jnp.exp(jnp.broadcast_to(run_s[:, span - 1 : span], (heads, LANES)))

    def values_of(head):
        return tok[:, pl.ds(pl.multiple_of(mine * bw + head * LANES, LANES), LANES)]

    def state_unit(p):
        tail = jnp.exp(run_t[span - 1 : span, :] - run_t[...])
        factor = jnp.zeros((span, LANES), f32)
        for a in range(per):
            inside = (lane >= a * key_size) & (lane < (a + 1) * key_size)
            factor = jnp.where(inside, tail[:, p * per + a : p * per + a + 1], factor)
        scaled = (ks[:, p * LANES : (p + 1) * LANES] * factor).T
        hi, lo = split(scaled)
        for a in range(per):
            head = p * per + a
            values = values_of(head)
            cut = slice(a * key_size, (a + 1) * key_size)
            block_state[head * key_size : (head + 1) * key_size, :] = (
                dot(hi, values) + dot(lo, values)
            )[cut]

    state_sent = []

    def pair_unit():
        pair_out[...] = block_state[...].astype(bf16)
        state_sent.append(send(pair_out, pair_in, st_send.at[0], st_recv.at[0], seq=partner))
        state_sent.append(send(retain_own, retain_in, st_send.at[1], st_recv.at[1], seq=partner))

    def chain_point(j):
        if j == 0:
            arrived(pair_in, st_recv.at[0])
            arrived(retain_in, st_recv.at[1])

        @pl.when(pair == j)
        def _():
            if j > 0:
                arrived(chain_in, st_recv.at[2])
            for head in range(heads):
                at_head = slice(head * key_size, (head + 1) * key_size)
                coming = carried[at_head, :] if j == 0 else chain_in[at_head, :].astype(f32)
                own_keep = retain_own[head : head + 1, :]
                other_keep = retain_in[head : head + 1, :]
                own = block_state[at_head, :]
                other = pair_in[at_head, :].astype(f32)
                is_odd = odd == 1
                prior[at_head, :] = jnp.where(is_odd, other_keep * coming + other, coming)
                if j < pairs - 1:
                    both = jnp.where(is_odd, own_keep * other + own, other_keep * own + other)
                    chain_out[at_head, :] = (own_keep * other_keep * coming + both).astype(bf16)
            if j < pairs - 1:
                send(chain_out, chain_in, st_send.at[2], st_recv.at[2], seq=ahead)

    def intra_unit(p):
        q_pair = qs[:, p * LANES : (p + 1) * LANES]
        k_hi, k_lo = split(ks[:, p * LANES : (p + 1) * LANES])
        for a in range(per):
            head = p * per + a
            inside = (lane >= a * key_size) & (lane < (a + 1) * key_size)
            q_hi, q_lo = split(jnp.where(inside, q_pair, 0.0))
            scores = dot(q_hi, k_hi, (1, 1)) + dot(q_hi, k_lo, (1, 1)) + dot(q_lo, k_hi, (1, 1))
            gaps = run_t[:, head : head + 1] - run_s[head : head + 1, :]
            scores = scores * jnp.where(row_t >= col_t, jnp.exp(jnp.minimum(gaps, 0.0)), 0.0)
            s_hi, s_lo = split(scores)
            values = values_of(head)
            intra[:, head * LANES : (head + 1) * LANES] = dot(s_hi, values) + dot(s_lo, values)

    def inter_unit(p):
        q_pair = qs[:, p * LANES : (p + 1) * LANES]
        s_hi, s_lo = split(prior[p * LANES : (p + 1) * LANES, :])
        for a in range(per):
            head = p * per + a
            cols = slice(head * LANES, (head + 1) * LANES)
            inside = (lane >= a * key_size) & (lane < (a + 1) * key_size)
            q_hi, q_lo = split(jnp.where(inside, q_pair, 0.0))
            carried_rows = dot(q_hi, s_hi) + dot(q_hi, s_lo) + dot(q_lo, s_hi)
            out = intra[:, cols] + jnp.exp(run_t[:, head : head + 1]) * carried_rows
            scale = lax.rsqrt(jnp.mean(out * out, axis=1, keepdims=True) + head_epsilon)
            hidden = values_of(head).astype(f32) + out * scale * out_gain[:, cols]
            intra[:, cols] = hidden
            student_out[:, cols] = hidden.astype(bf16)

    def gather_unit(b, t, members):
        def gather(i, _):
            off = pl.multiple_of(i * step_cols, step_cols)
            for h in range(cuts):
                got = [
                    rows[t][spot(rel), h, :, :, pl.ds(off, step_cols)].astype(f32).reshape(size_of[t], step_cols)
                    for rel in members
                ]
                got = jnp.concatenate(got, axis=0) if len(got) > 1 else got[0]
                lhs[0 : got.shape[0], pl.ds(h * cut_cols + off, step_cols)] = got.astype(bf16)
            return 0

        lax.fori_loop(0, cut_cols // step_cols, gather, 0)

    tile = min(256, ff)

    def hidden_unit(b, m, i):
        if b == 0 and i == 0:
            loads[3].wait()
            loads[4].wait()
        cols = slice(i * tile, (i + 1) * tile)
        a = lhs[0:m, :]
        gated = dot(a, gate[:, cols])
        upped = dot(a, up[:, cols])
        silu = gated / (1.0 + jnp.exp(-gated))
        hid[b][:, cols] = (silu * upped).astype(bf16)

    def down_unit(b, t, members, h):
        if b == 0 and h == 0:
            loads[5].wait()

        def columns(i, _):
            off = pl.multiple_of(i * step_cols, step_cols)
            got = dot(hid[b][...], down[:, pl.ds(h * cut_cols + off, step_cols)])
            for j, rel in enumerate(members):
                piece = got[j * size_of[t] : (j + 1) * size_of[t]].reshape(parts[t], SUB, step_cols)
                part[t][spot(rel), h, :, :, pl.ds(off, step_cols)] = piece.astype(bf16)
            return 0

        lax.fori_loop(0, cut_cols // step_cols, columns, 0)

    near = [0] + [s * k for k in range(1, half - 1) for s in (1, -1)]
    last = [half - 1, 1 - half, half]
    batches = [(0, near), (0, last)] + [(t, near + last) for t in splits if t > 0]

    def ag_of(t, members):
        found = []
        for rel in members:
            if rel > 0:
                found += [("ag", t, rel, w) for w in range(cuts if rel < half else cuts // 2)]
        return found

    per_cut = groups // cuts

    def finals(t):
        return [("rs", t, 1, w) for w in range(cuts)]

    def final_step(t, j):
        need(("rs", t, 1, cuts - 1 - j))
        need(("rs", t, 1, j))
        here = [q for q in range(groups) if q // per_cut in (j, cuts - 1 - j)]
        for q in here:
            h = q // per_cut
            cols = pl.ds((q % per_cut) * bw, bw)
            total = part[t][0, h, :, :, cols].astype(f32)
            total = total + inbox[t][0, 1, h, :, :, cols].astype(f32)
            total = total + inbox[t][1, 1, h, :, :, cols].astype(f32)
            expert_out[t][q] = total.astype(bf16)
        for q in here:
            shift = lax.rem(q + groups - mine, groups)

            @pl.when(mine != q)
            def _(q=q, shift=shift):
                send(expert_out[t].at[q], expert_in[t].at[shift], ex_send.at[t], ex_recv.at[t], expert=q)

    def final_sum(t):
        for j in range(cuts // 2):
            final_step(t, j)
        expert_in[t][0] = expert_out[t][mine]

    def mixed_of(t, i):
        cols = slice(i * step_cols, (i + 1) * step_cols)
        got = [
            expert_in[t][shift, :, :, cols].astype(f32).reshape(size_of[t], step_cols)
            for shift in range(groups)
        ]
        got = jnp.concatenate(got, axis=0).astype(bf16)
        return dot(mix_high[t][...], got) + dot(mix_low[t][...], got)

    def take_in(t):
        arrived(expert_in[t].at[1:groups], ex_recv.at[t])

    def mix_unit():
        for t in splits[:-1]:
            take_in(t)
        for i in range(bw // step_cols):
            cols = slice(i * step_cols, (i + 1) * step_cols)
            total = tok[:, pl.ds(pl.multiple_of(mine * bw + i * step_cols, LANES), step_cols)].astype(f32)
            for t in splits[:-1]:
                total = total + mixed_of(t, i)
            teacher[:, cols] = total

    plan.unit("keys", 0.8, keys_unit, start=3.0)
    plan.unit("decay", 0.4, decay_unit)
    state_names = []
    for p in range(heads // per):
        state_names.append(f"state{p}")
        plan.unit(f"state{p}", 0.35, functools.partial(state_unit, p), after=["keys", "decay"])
    plan.unit("pair", 0.3, pair_unit, after=state_names)
    for j in range(pairs):
        before_it = ["pair"] if j == 0 else [f"chain{j - 1}"]
        plan.unit(f"chain{j}", 0.2, functools.partial(chain_point, j), after=before_it, start=22.0 + 12.0 * j)
    plan.unit("queries", 0.8, queries_unit, start=4.0)

    def load_down():
        loads[5].start()

    plan.unit("down load", 0.0, load_down, start=8.0)
    for b, (t, members) in enumerate(batches):
        m = len(members) * size_of[t]
        share = ff / 1024
        plan.unit(
            f"gather{b}",
            0.4,
            functools.partial(
                lambda b, t, members: ([need(x) for x in ag_of(t, members)], gather_unit(b, t, members)),
                b,
                t,
                members,
            ),
            after=[f"hidden{b - 1}.{ff // tile - 1}"] if b else [],
            messages=ag_of(t, members),
        )
        for i in range(ff // tile):
            plan.unit(
                f"hidden{b}.{i}",
                max(0.85, m * 0.0054),
                functools.partial(hidden_unit, b, m, i),
                after=[f"gather{b}"] + ([f"hidden{b}.{i - 1}"] if i else []),
            )
        for h in range(cuts):
            plan.unit(
                f"down{b}.{h}",
                (2.1 + 0.005 * m) * share / cuts,
                functools.partial(down_unit, b, t, members, h),
                after=[f"hidden{b}.{ff // tile - 1}", "down load"],
            )
    plan.unit("mixing", 1.0, mixing_unit)
    for p in range(heads // per):
        plan.unit(f"intra{p}", 0.6, functools.partial(intra_unit, p), after=["keys", "queries", "decay"])
    for p in range(heads // per):
        plan.unit(
            f"inter{p}", 0.35, functools.partial(inter_unit, p), after=[f"intra{p}", f"chain{pairs - 1}"]
        )

    def ring(kind, t, k, which, needs=()):
        prev = (kind, t, k - 1 if kind == "ag" else k + 1, which)
        message = (kind, t, k, which)
        plan.message(
            message,
            size_of[t] * cut_cols * 2,
            functools.partial(go, message),
            prev if prev in plan.arrival else None,
            needs,
        )

    gathers = [
        [(t, k, w) for k in range(1, half + 1) for w in range(cuts if k < half else cuts // 2)] for t in splits
    ]
    early = gathers[0]
    rest = [x for more in gathers[1:] for x in more]
    for i, x in enumerate(early):
        ring("ag", *x)
        if i in (cuts - 1, len(early) - cuts // 2 - 1) and rest:
            for _ in range(cuts // 2):
                ring("ag", *rest.pop(0))
    for x in rest:
        ring("ag", *x)
    for t in splits:
        for k in range(half, 0, -1):
            for which in list(range(cuts // 2, cuts)) * (k < half) + list(range(cuts // 2)):
                here = [b for b, (u, members) in enumerate(batches) if u == t and k in [abs(r) for r in members]]
                both = sorted({which, cuts - 1 - which})
                ring("rs", t, k, which, [f"down{b}.{h}" for b in here for h in both])
        if t < len(parts) - 1:
            plan.unit(
                f"final{t}",
                0.2,
                functools.partial(final_sum, t),
                messages=finals(t),
                start=max(plan.arrival[m] for m in finals(t)) + 6.0,
                after=[f"down{b}.{h}" for b, (u, _) in enumerate(batches) if u == t for h in range(cuts)],
            )
    stores = [
        pltpu.make_async_copy(teacher_out, teacher_hbm, load_sem.at[0]),
        pltpu.make_async_copy(student_out, student_hbm, load_sem.at[1]),
    ]

    plan.unit(
        "store", 0.0, stores[1].start, after=[f"inter{p}" for p in range(heads // per)]
    )
    if len(parts) > 1:
        plan.unit("mix", 0.4, mix_unit, after=[f"final{len(parts) - 2}", "mixing"], start=max(plan.arrival[m] for m in finals(len(parts) - 2)) + 11.0)
    end = max(plan.arrival[m] for m in finals(len(parts) - 1))
    plan.fill(end)
    plan.drain()

    t = len(parts) - 1
    final_sum(t)
    take_in(t)
    gap_sum = jnp.zeros((span, LANES), f32)
    for i in range(bw // step_cols):
        cols = slice(i * step_cols, (i + 1) * step_cols)
        hidden = teacher[:, cols] + mixed_of(t, i)
        teacher_out[:, cols] = hidden.astype(bf16)
        gap = intra[:, cols] - hidden
        gap = gap * gap
        for c in range(step_cols // LANES):
            gap_sum = gap_sum + gap[:, c * LANES : (c + 1) * LANES]
    stores[0].start()
    loss_all[mine] = dot(jnp.ones((SUB, LANES), f32), gap_sum, (1, 1), exact)
    for shift in range(1, groups):
        peer = lax.rem(mine + shift, groups)
        send(loss_all.at[mine], loss_all.at[mine], lo_send, lo_recv, expert=peer)
    for t in splits:
        arrived(rows[t].at[0 : n - 1], ag_send.at[t])
        arrived(part[t].at[0 : n - 1], rs_send.at[t])
        arrived(expert_out[t].at[1:groups], ex_send.at[t])
    for copy in state_sent:
        copy.wait_send()

    @pl.when(pair < pairs - 1)
    def _():
        pltpu.make_async_copy(chain_out, chain_out, st_send.at[2]).wait()

    for copy in stores:
        copy.wait()
    arrived(loss_all.at[1:groups], lo_send)
    arrived(loss_all.at[1:groups], lo_recv)
    total = loss_all[0]
    for q in range(1, groups):
        total = total + loss_all[q]
    loss_out[...] = total / width


def result_kernel(teacher_in, student_in, loss_in, teacher_out, student_out, loss_out):
    teacher_out[...] = teacher_in[...]
    student_out[...] = student_in[...]
    loss_out[...] = loss_in[0:1, :]


def on_device(
    order,
    tokens,
    norm_gain,
    router_weight,
    expert_ids,
    gate_weight,
    up_weight,
    down_weight,
    query_weight,
    key_weight,
    log_decay,
    carried_state,
    out_gain,
):
    span, width = tokens.shape
    experts = router_weight.shape[1]
    groups = lax.axis_size("expert")
    cap = 7 * expert_ids.shape[1] * span // (8 * experts)
    g = -(-cap // SUB)
    n = len(order)
    half = n // 2
    ff = gate_weight.shape[2]
    bw = width // groups
    heads, key_size, feats = carried_state.shape
    keys = heads * key_size
    hbm = pl.BlockSpec(memory_space=pl.ANY)
    vmem = pl.BlockSpec(memory_space=pltpu.VMEM)
    dma = pltpu.SemaphoreType.DMA
    parts = (g - g // 2, g // 2) if g > 1 else (g,)
    sizes = [p * SUB for p in parts]
    near, last = n - 3, 3
    counts = [near * sizes[0], last * sizes[0]] + [n * size for size in sizes[1:]]

    cuts = min(4, groups) if n <= 8 else 2
    cut_cols = width // cuts

    steps = (half - 1) * cuts + cuts // 2

    scratch = [
        pltpu.VMEM((1, width), f32),
        pltpu.VMEM((experts, width), bf16),
        pltpu.VMEM(expert_ids.shape[::-1], jnp.int32),
        pltpu.VMEM(log_decay.shape, f32),
        pltpu.VMEM((keys, feats), f32),
        pltpu.VMEM((1, bw), f32),
        pltpu.VMEM((span, bw), bf16),
        pltpu.VMEM((span, bw), bf16),
        pltpu.VMEM((span, width), bf16),
        pltpu.VMEM((width, ff), bf16),
        pltpu.VMEM((width, ff), bf16),
        pltpu.VMEM((ff, width), bf16),
        pltpu.VMEM((width, keys), bf16),
        pltpu.VMEM((width, keys), bf16),
        pltpu.VMEM((span, width), bf16),
        pltpu.VMEM((max(counts), width), bf16),
        pltpu.VMEM((span, keys), f32),
        pltpu.VMEM((span, keys), f32),
        pltpu.VMEM((heads, span), f32),
        pltpu.VMEM((span, heads), f32),
        pltpu.VMEM((heads, LANES), f32),
        pltpu.VMEM((keys, feats), f32),
        pltpu.VMEM((keys, feats), f32),
        pltpu.VMEM((keys, feats), bf16),
        pltpu.VMEM((keys, feats), bf16),
        pltpu.VMEM((heads, LANES), f32),
        pltpu.VMEM((keys, feats), bf16),
        pltpu.VMEM((keys, feats), bf16),
        pltpu.VMEM((span, bw), f32),
        pltpu.VMEM((span, bw), f32),
        pltpu.VMEM((span, LANES), f32),
        pltpu.VMEM((groups, SUB, span), f32),
        [pltpu.VMEM((n, cuts, p, SUB, cut_cols), bf16) for p in parts],
        [pltpu.VMEM((n, cuts, p, SUB, cut_cols), bf16) for p in parts],
        [pltpu.VMEM((2, half + 1, cuts, p, SUB, cut_cols), bf16) for p in parts],
        [pltpu.VMEM((count, ff), bf16) for count in counts],
        [pltpu.VMEM((span, groups * size), bf16) for size in sizes],
        [pltpu.VMEM((span, groups * size), bf16) for size in sizes],
        [pltpu.VMEM((groups, p, SUB, bw), bf16) for p in parts],
        [pltpu.VMEM((groups, p, SUB, bw), bf16) for p in parts],
        dma((12,)),
        dma((len(parts),)),
        dma((len(parts), steps)),
        dma((len(parts),)),
        dma((len(parts), steps)),
        dma((3,)),
        dma((3,)),
        dma((len(parts),)),
        dma((len(parts),)),
        dma,
        dma,
    ]
    teacher, student, loss = pl.pallas_call(
        functools.partial(layer_kernel, order, cap, parts, cuts),
        out_shape=(
            jax.ShapeDtypeStruct((span, bw), bf16),
            jax.ShapeDtypeStruct((span, bw), bf16),
            jax.ShapeDtypeStruct((SUB, span), f32),
        ),
        in_specs=[hbm] * 12,
        out_specs=(hbm, hbm, vmem),
        scratch_shapes=scratch,
        compiler_params=pltpu.CompilerParams(
            collective_id=0, has_side_effects=True, vmem_limit_bytes=60 * 1024 * 1024
        ),
        name="layer",
    )(
        tokens,
        norm_gain.reshape(1, width),
        router_weight.T,
        expert_ids.T,
        gate_weight.reshape(width, ff),
        up_weight.reshape(width, ff),
        down_weight.reshape(ff, width),
        query_weight,
        key_weight,
        log_decay,
        carried_state.reshape(keys, feats),
        out_gain.reshape(1, bw),
    )
    teacher, student, loss = pl.pallas_call(
        result_kernel,
        out_shape=(
            jax.ShapeDtypeStruct((span, bw), bf16),
            jax.ShapeDtypeStruct((span, bw), bf16),
            jax.ShapeDtypeStruct((1, span), f32),
        ),
        in_specs=[vmem, vmem, vmem],
        out_specs=(vmem, vmem, vmem),
        name="result",
    )(teacher, student, loss)
    return teacher, student, loss.reshape(span)


def solution(mesh):
    return jax.shard_map(
        functools.partial(on_device, tuple(ring_order(mesh))),
        mesh=mesh,
        in_specs=(
            P("seq", None),
            P(),
            P(),
            P("seq", None),
            P("expert", None, "seq"),
            P("expert", None, "seq"),
            P("expert", "seq", None),
            P(None, "expert"),
            P(None, "expert"),
            P("expert", "seq"),
            P("expert", None, None),
            P("expert"),
        ),
        out_specs=(P("seq", "expert"), P("seq", "expert"), P("seq")),
        check_vma=False,
    )
```

time: 106 us -> 92.1 us (0.87)
  local copies, waits for them, and re-layouts: 8.11 us -> 0 us
  Pallas kernels: 96.6 us -> 91.3 us
    unnamed x4 -> x0, local copies, waits for them, and re-layouts: 6.91 us -> none
    pallas_call x1 -> x2, Pallas kernels: 96.6 us -> 91.3 us  [the longest x1 89.5 us: on_device(): pl.pallas_call(functools.partial(layer_kernel, order, cap, parts, cuts),...]
    squeeze x1 -> x0, local copies, waits for them, and re-layouts: 1.2 us -> none  [on_device(): return (teacher, student, loss[0])]
where the time goes in v1:
time: 92.1 us; the launch traced here: 92 us
  Pallas kernels  91.3 us (99%)
    pallas_call x1, Pallas kernels, on_device(): pl.pallas_call(functools.partial(layer_kernel, order, cap, parts, cuts),...  89.5 us

profile of v1, /device:TPU:0, one launch (start us, length us, event | category | flops | bytes accessed | tf_op | source)
XLA Modules:
  0.0 92.0 jit_solution(11205273309181001830)
XLA Ops:
  0.6 89.5 %layer.1 = (bf16[128,1024]{1,0:T(8,128)(2,1)}, bf16[128,1024]{1,0:T(8,128)(2,1)}, f32[8,128]{1,0:T(8,128)}) custom-call(bf16[128,4096]{1,0:T(8,128)(2,1)} %tok_hbm.1, f32[1,4096]{1,0:T(1,128)} %bitcast.14, bf16[4,4096]{1,0:T(4,128)(2,1)} %bitcast.13, s32[2,128]{1,0:T(2,128)} %bitcast.16, bf16[4096,1024]{1,0:T(8,128)(2,1)} %bitcast.9, ...), custom_call_target="tpu_custom_call" | custom-call | tf_op jit(solution)/shard_map/layer/pallas_call | solution.py:839
  90.1 1.8 %result.1 = (bf16[128,1024]{1,0:T(8,128)(2,1)}, bf16[128,1024]{1,0:T(8,128)(2,1)}, f32[1,128]{1,0:T(1,128)}) custom-call(bf16[128,1024]{1,0:T(8,128)(2,1)} %get-tuple-element.9.teacher_in, bf16[128,1024]{1,0:T(8,128)(2,1)} %get-tuple-element.10.student_in, f32[8,128]{1,0:T(8,128)} %get-tuple-element.11.loss_in), custom_call_target="tpu_custom_call" | custom-call | tf_op jit(solution)/shard_map/result/pallas_call | solution.py:867

commit v2 on v1

--- a/solution.py
+++ b/solution.py
@@ -136,8 +136,8 @@
     decay_hbm,
     carried_hbm,
     out_gain_hbm,
-    teacher_hbm,
-    student_hbm,
+    teacher_out,
+    student_out,
     loss_out,
     gain,
     router,
@@ -145,8 +145,6 @@
     decay,
     carried,
     out_gain,
-    teacher_out,
-    student_out,
     tok,
     gate,
     up,
@@ -167,6 +165,8 @@
     retain_in,
     chain_out,
     chain_in,
+    relay_out,
+    relay_in,
     intra,
     teacher,
     slot_s,
@@ -433,36 +433,58 @@
                 dot(hi, values) + dot(lo, values)
             )[cut]
 
-    state_sent = []
+    hk = heads * key_size // 2
+    half_heads = heads // 2
+    own_half = pl.ds(pl.multiple_of(odd * hk, key_size), hk)
+    other_half = pl.ds(pl.multiple_of((1 - odd) * hk, key_size), hk)
+    gives = (pair < pairs - 1) | (odd == 0)
 
     def pair_unit():
-        pair_out[...] = block_state[...].astype(bf16)
-        state_sent.append(send(pair_out, pair_in, st_send.at[0], st_recv.at[0], seq=partner))
-        state_sent.append(send(retain_own, retain_in, st_send.at[1], st_recv.at[1], seq=partner))
+        pair_out[...] = block_state[other_half, :].astype(bf16)
+
+        @pl.when(gives)
+        def _():
+            send(pair_out, pair_in, st_send.at[0], st_recv.at[0], seq=partner)
+            send(retain_own, retain_in, st_send.at[1], st_recv.at[1], seq=partner)
 
     def chain_point(j):
-        if j == 0:
+        last_pair = j == pairs - 1
+
+        def pair_wait():
             arrived(pair_in, st_recv.at[0])
             arrived(retain_in, st_recv.at[1])
 
         @pl.when(pair == j)
         def _():
+            if last_pair:
+                pl.when(odd == 1)(pair_wait)
+            else:
+                pair_wait()
             if j > 0:
                 arrived(chain_in, st_recv.at[2])
-            for head in range(heads):
-                at_head = slice(head * key_size, (head + 1) * key_size)
-                coming = carried[at_head, :] if j == 0 else chain_in[at_head, :].astype(f32)
-                own_keep = retain_own[head : head + 1, :]
-                other_keep = retain_in[head : head + 1, :]
-                own = block_state[at_head, :]
-                other = pair_in[at_head, :].astype(f32)
-                is_odd = odd == 1
-                prior[at_head, :] = jnp.where(is_odd, other_keep * coming + other, coming)
-                if j < pairs - 1:
-                    both = jnp.where(is_odd, own_keep * other + own, other_keep * own + other)
-                    chain_out[at_head, :] = (own_keep * other_keep * coming + both).astype(bf16)
-            if j < pairs - 1:
+            is_odd = odd == 1
+            for i in range(half_heads):
+                rows_i = slice(i * key_size, (i + 1) * key_size)
+                at_i = pl.ds(pl.multiple_of(odd * hk + i * key_size, key_size), key_size)
+                head = pl.ds(odd * half_heads + i, 1)
+                coming = carried[at_i, :] if j == 0 else chain_in[rows_i, :].astype(f32)
+                own_keep = retain_own[head, :]
+                other_keep = retain_in[head, :]
+                own = block_state[at_i, :]
+                other = pair_in[rows_i, :].astype(f32)
+                later = jnp.where(is_odd, other_keep * coming + other, own_keep * coming + own)
+                prior[at_i, :] = jnp.where(is_odd, later, coming)
+                relay_out[rows_i, :] = jnp.where(is_odd, coming, later).astype(bf16)
+                if not last_pair:
+                    beyond = jnp.where(is_odd, own_keep * later + own, other_keep * later + other)
+                    chain_out[rows_i, :] = beyond.astype(bf16)
+            send(relay_out, relay_in, st_send.at[3], st_recv.at[3], seq=partner)
+            if not last_pair:
                 send(chain_out, chain_in, st_send.at[2], st_recv.at[2], seq=ahead)
+
+    def relay_unit():
+        arrived(relay_in, st_recv.at[3])
+        prior[other_half, :] = relay_in[...].astype(f32)
 
     def intra_unit(p):
         q_pair = qs[:, p * LANES : (p + 1) * LANES]
@@ -605,6 +627,7 @@
     for j in range(pairs):
         before_it = ["pair"] if j == 0 else [f"chain{j - 1}"]
         plan.unit(f"chain{j}", 0.2, functools.partial(chain_point, j), after=before_it, start=22.0 + 12.0 * j)
+    plan.unit("relay", 0.1, relay_unit, after=[f"chain{pairs - 1}"], start=34.0 + 12.0 * (pairs - 1))
     plan.unit("queries", 0.8, queries_unit, start=4.0)
 
     def load_down():
@@ -645,7 +668,7 @@
         plan.unit(f"intra{p}", 0.6, functools.partial(intra_unit, p), after=["keys", "queries", "decay"])
     for p in range(heads // per):
         plan.unit(
-            f"inter{p}", 0.35, functools.partial(inter_unit, p), after=[f"intra{p}", f"chain{pairs - 1}"]
+            f"inter{p}", 0.35, functools.partial(inter_unit, p), after=[f"intra{p}", "relay"]
         )
 
     def ring(kind, t, k, which, needs=()):
@@ -686,14 +709,6 @@
                 start=max(plan.arrival[m] for m in finals(t)) + 6.0,
                 after=[f"down{b}.{h}" for b, (u, _) in enumerate(batches) if u == t for h in range(cuts)],
             )
-    stores = [
-        pltpu.make_async_copy(teacher_out, teacher_hbm, load_sem.at[0]),
-        pltpu.make_async_copy(student_out, student_hbm, load_sem.at[1]),
-    ]
-
-    plan.unit(
-        "store", 0.0, stores[1].start, after=[f"inter{p}" for p in range(heads // per)]
-    )
     if len(parts) > 1:
         plan.unit("mix", 0.4, mix_unit, after=[f"final{len(parts) - 2}", "mixing"], start=max(plan.arrival[m] for m in finals(len(parts) - 2)) + 11.0)
     end = max(plan.arrival[m] for m in finals(len(parts) - 1))
@@ -712,7 +727,6 @@
         gap = gap * gap
         for c in range(step_cols // LANES):
             gap_sum = gap_sum + gap[:, c * LANES : (c + 1) * LANES]
-    stores[0].start()
     loss_all[mine] = dot(jnp.ones((SUB, LANES), f32), gap_sum, (1, 1), exact)
     for shift in range(1, groups):
         peer = lax.rem(mine + shift, groups)
@@ -721,27 +735,36 @@
         arrived(rows[t].at[0 : n - 1], ag_send.at[t])
         arrived(part[t].at[0 : n - 1], rs_send.at[t])
         arrived(expert_out[t].at[1:groups], ex_send.at[t])
-    for copy in state_sent:
-        copy.wait_send()
+    arrived(relay_out, st_send.at[3])
+
+    @pl.when(gives)
+    def _():
+        arrived(pair_out, st_send.at[0])
+        arrived(retain_own, st_send.at[1])
 
     @pl.when(pair < pairs - 1)
     def _():
-        pltpu.make_async_copy(chain_out, chain_out, st_send.at[2]).wait()
-
-    for copy in stores:
-        copy.wait()
+        arrived(chain_out, st_send.at[2])
+
     arrived(loss_all.at[1:groups], lo_send)
     arrived(loss_all.at[1:groups], lo_recv)
     total = loss_all[0]
     for q in range(1, groups):
         total = total + loss_all[q]
-    loss_out[...] = total / width
-
-
-def result_kernel(teacher_in, student_in, loss_in, teacher_out, student_out, loss_out):
-    teacher_out[...] = teacher_in[...]
-    student_out[...] = student_in[...]
-    loss_out[...] = loss_in[0:1, :]
+    loss_out[...] = total[0:1, :] / width
+
+
+def result_kernel(teacher_in, student_in, loss_in, teacher_out, student_out, loss_out, sems):
+    copies = [
+        pltpu.make_async_copy(src, dst, sems.at[i])
+        for i, (src, dst) in enumerate(
+            ((teacher_in, teacher_out), (student_in, student_out), (loss_in, loss_out))
+        )
+    ]
+    for copy in copies:
+        copy.start()
+    for copy in copies:
+        copy.wait()
 
 
 def on_device(
@@ -790,8 +813,6 @@
         pltpu.VMEM(log_decay.shape, f32),
         pltpu.VMEM((keys, feats), f32),
         pltpu.VMEM((1, bw), f32),
-        pltpu.VMEM((span, bw), bf16),
-        pltpu.VMEM((span, bw), bf16),
         pltpu.VMEM((span, width), bf16),
         pltpu.VMEM((width, ff), bf16),
         pltpu.VMEM((width, ff), bf16),
@@ -807,11 +828,13 @@
         pltpu.VMEM((heads, LANES), f32),
         pltpu.VMEM((keys, feats), f32),
         pltpu.VMEM((keys, feats), f32),
-        pltpu.VMEM((keys, feats), bf16),
-        pltpu.VMEM((keys, feats), bf16),
+        pltpu.VMEM((keys // 2, feats), bf16),
+        pltpu.VMEM((keys // 2, feats), bf16),
         pltpu.VMEM((heads, LANES), f32),
-        pltpu.VMEM((keys, feats), bf16),
-        pltpu.VMEM((keys, feats), bf16),
+        pltpu.VMEM((keys // 2, feats), bf16),
+        pltpu.VMEM((keys // 2, feats), bf16),
+        pltpu.VMEM((keys // 2, feats), bf16),
+        pltpu.VMEM((keys // 2, feats), bf16),
         pltpu.VMEM((span, bw), f32),
         pltpu.VMEM((span, bw), f32),
         pltpu.VMEM((span, LANES), f32),
@@ -829,8 +852,8 @@
         dma((len(parts), steps)),
         dma((len(parts),)),
         dma((len(parts), steps)),
-        dma((3,)),
-        dma((3,)),
+        dma((4,)),
+        dma((4,)),
         dma((len(parts),)),
         dma((len(parts),)),
         dma,
@@ -839,12 +862,12 @@
     teacher, student, loss = pl.pallas_call(
         functools.partial(layer_kernel, order, cap, parts, cuts),
         out_shape=(
-            jax.ShapeDtypeStruct((span, bw), bf16),
-            jax.ShapeDtypeStruct((span, bw), bf16),
-            jax.ShapeDtypeStruct((SUB, span), f32),
+            pltpu.VMEM((span, bw), bf16),
+            pltpu.VMEM((span, bw), bf16),
+            pltpu.VMEM((1, span), f32),
         ),
         in_specs=[hbm] * 12,
-        out_specs=(hbm, hbm, vmem),
+        out_specs=(vmem, vmem, vmem),
         scratch_shapes=scratch,
         compiler_params=pltpu.CompilerParams(
             collective_id=0, has_side_effects=True, vmem_limit_bytes=60 * 1024 * 1024
@@ -872,9 +895,10 @@
             jax.ShapeDtypeStruct((1, span), f32),
         ),
         in_specs=[vmem, vmem, vmem],
-        out_specs=(vmem, vmem, vmem),
+        out_specs=(hbm, hbm, hbm),
+        scratch_shapes=[dma((3,))],
         name="result",
-    )(teacher, student, loss)
+    )(*(pltpu.with_memory_space_constraint(x, pltpu.VMEM) for x in (teacher, student, loss)))
     return teacher, student, loss.reshape(span)
 
 

time: 92.1 us -> 87.8 us (0.953)
  Pallas kernels: 91.3 us -> 86.9 us
    pallas_call x1, Pallas kernels: 89.5 us -> 86.1 us  [on_device(): pl.pallas_call(functools.partial(layer_kernel, order, cap, parts, cuts),...]
    pallas_call x1, Pallas kernels: 1.84 us -> 0.82 us  [on_device(): pl.pallas_call(result_kernel, out_shape=(jax.ShapeDtypeStruct((span, bw),...]
where the time goes in v2:
time: 87.8 us; the launch traced here: 87.7 us
  Pallas kernels  86.9 us (99%)
    pallas_call x1, Pallas kernels, on_device(): pl.pallas_call(functools.partial(layer_kernel, order, cap, parts, cuts),...  86.1 us

profile of v2, /device:TPU:0, one launch (start us, length us, event | category | flops | bytes accessed | tf_op | source)
XLA Modules:
  0.0 87.7 jit_solution(2299444998575862568)
XLA Ops:
  0.6 86.1 %layer.1 = (bf16[128,1024]{1,0:T(8,128)(2,1)S(1)}, bf16[128,1024]{1,0:T(8,128)(2,1)S(1)}, f32[1,128]{1,0:T(1,128)S(1)}) custom-call(bf16[128,4096]{1,0:T(8,128)(2,1)} %tok_hbm.1, f32[1,4096]{1,0:T(1,128)} %bitcast.14, bf16[4,4096]{1,0:T(4,128)(2,1)} %bitcast.13, s32[2,128]{1,0:T(2,128)} %bitcast.16, bf16[4096,1024]{1,0:T(8,128)(2,1)} %bitcast.9, ...), custom_call_target="tpu_custom_call" | custom-call | tf_op jit(solution)/shard_map/layer/pallas_call | solution.py:862
  86.7 0.8 result.1

commit v3 on v2

--- a/solution.py
+++ b/solution.py
@@ -190,6 +190,7 @@
     ex_recv,
     lo_send,
     lo_recv,
+    ow_recv,
 ):
     n = len(order)
     half = n // 2
@@ -252,8 +253,11 @@
         copy.start()
 
     barrier = pltpu.get_barrier_semaphore()
-    for there in (right, left, partner, ahead, behind):
+    for there in (partner, ahead, behind):
         pl.semaphore_signal(barrier, inc=1, device_id={"seq": there}, device_id_type=MESH)
+    for there in (right, left):
+        for q in range(groups):
+            pl.semaphore_signal(barrier, inc=1, device_id={"seq": there, "expert": q}, device_id_type=MESH)
     for shift in range(1, groups):
         peer = lax.rem(mine + shift, groups)
         pl.semaphore_signal(barrier, inc=1, device_id={"expert": peer}, device_id_type=MESH)
@@ -310,7 +314,7 @@
     loads[4].start()
     for copy in loads[small + 2 :]:
         copy.wait()
-    pl.semaphore_wait(barrier, 5 + groups - 1)
+    pl.semaphore_wait(barrier, 3 + 2 * groups + groups - 1)
     ready_cuts = set()
 
     def dispatch(h):
@@ -324,6 +328,7 @@
 
     plan = Plan()
     waited = set()
+    per_cut = groups // cuts
 
     def spot(rel):
         return rel % n
@@ -372,6 +377,12 @@
                         return 0
 
                     lax.fori_loop(0, cut_cols // step_cols, add_cols, 0)
+                if k == 1 and t == len(parts) - 1:
+                    for q in range(h * per_cut, (h + 1) * per_cut):
+                        piece = part[t].at[rel, h, :, :, pl.ds((q - h * per_cut) * bw, bw)]
+                        there = expert_in[t].at[lax.rem(q + groups - mine, groups), side]
+                        send(piece, there, rs_send.at[t], ex_recv.at[t], seq=sides[side], expert=q)
+                    continue
                 src = part[t].at[rel, h]
                 dst = inbox[t].at[side, k, h]
                 out = rs_send.at[t]
@@ -567,7 +578,19 @@
                 found += [("ag", t, rel, w) for w in range(cuts if rel < half else cuts // 2)]
         return found
 
-    per_cut = groups // cuts
+    def own_unit(t):
+        for q in range(groups):
+            h = q // per_cut
+            shift = lax.rem(q + groups - mine, groups)
+            cols = pl.ds((q - h * per_cut) * bw, bw)
+
+            @pl.when(mine != q)
+            def _(q=q, h=h, shift=shift, cols=cols):
+                send(part[t].at[0, h, :, :, cols], expert_in[t].at[shift, 2], ex_send.at[t], ow_recv, expert=q)
+
+            @pl.when(mine == q)
+            def _(q=q, h=h, cols=cols):
+                expert_in[t][0, 2] = part[t][0, h, :, :, cols]
 
     def finals(t):
         return [("rs", t, 1, w) for w in range(cuts)]
@@ -597,12 +620,23 @@
 
     def mixed_of(t, i):
         cols = slice(i * step_cols, (i + 1) * step_cols)
-        got = [
-            expert_in[t][shift, :, :, cols].astype(f32).reshape(size_of[t], step_cols)
-            for shift in range(groups)
-        ]
+        got = []
+        for shift in range(groups):
+            if t < len(parts) - 1:
+                one = expert_in[t][shift, :, :, cols].astype(f32)
+            else:
+                one = expert_in[t][shift, 2, :, :, cols].astype(f32)
+                one = one + expert_in[t][shift, 0, :, :, cols].astype(f32)
+                one = one + expert_in[t][shift, 1, :, :, cols].astype(f32)
+                one = one.astype(bf16).astype(f32)
+            got.append(one.reshape(size_of[t], step_cols))
         got = jnp.concatenate(got, axis=0).astype(bf16)
         return dot(mix_high[t][...], got) + dot(mix_low[t][...], got)
+
+    def take_last():
+        t = len(parts) - 1
+        arrived(expert_in[t].at[1:groups, 2], ow_recv)
+        arrived(expert_in[t].at[:, 0:2], ex_recv.at[t])
 
     def take_in(t):
         arrived(expert_in[t].at[1:groups], ex_recv.at[t])
@@ -709,6 +743,14 @@
                 start=max(plan.arrival[m] for m in finals(t)) + 6.0,
                 after=[f"down{b}.{h}" for b, (u, _) in enumerate(batches) if u == t for h in range(cuts)],
             )
+    t = len(parts) - 1
+    plan.unit(
+        "own",
+        0.2,
+        functools.partial(own_unit, t),
+        after=[f"down{b}.{h}" for b, (u, _) in enumerate(batches) if u == t for h in range(cuts)],
+        start=max(plan.arrival[m] for m in finals(t)) - 12.0,
+    )
     if len(parts) > 1:
         plan.unit("mix", 0.4, mix_unit, after=[f"final{len(parts) - 2}", "mixing"], start=max(plan.arrival[m] for m in finals(len(parts) - 2)) + 11.0)
     end = max(plan.arrival[m] for m in finals(len(parts) - 1))
@@ -716,8 +758,7 @@
     plan.drain()
 
     t = len(parts) - 1
-    final_sum(t)
-    take_in(t)
+    take_last()
     gap_sum = jnp.zeros((span, LANES), f32)
     for i in range(bw // step_cols):
         cols = slice(i * step_cols, (i + 1) * step_cols)
@@ -734,7 +775,7 @@
     for t in splits:
         arrived(rows[t].at[0 : n - 1], ag_send.at[t])
         arrived(part[t].at[0 : n - 1], rs_send.at[t])
-        arrived(expert_out[t].at[1:groups], ex_send.at[t])
+        arrived(expert_out[t].at[1:groups] if t < len(parts) - 1 else expert_in[t].at[1:groups, 2], ex_send.at[t])
     arrived(relay_out, st_send.at[3])
 
     @pl.when(gives)
@@ -845,8 +886,9 @@
         [pltpu.VMEM((count, ff), bf16) for count in counts],
         [pltpu.VMEM((span, groups * size), bf16) for size in sizes],
         [pltpu.VMEM((span, groups * size), bf16) for size in sizes],
-        [pltpu.VMEM((groups, p, SUB, bw), bf16) for p in parts],
-        [pltpu.VMEM((groups, p, SUB, bw), bf16) for p in parts],
+        [pltpu.VMEM((groups, p, SUB, bw), bf16) for p in parts[:-1]],
+        [pltpu.VMEM((groups, p, SUB, bw), bf16) for p in parts[:-1]]
+        + [pltpu.VMEM((groups, 3, parts[-1], SUB, bw), bf16)],
         dma((12,)),
         dma((len(parts),)),
         dma((len(parts), steps)),
@@ -856,6 +898,7 @@
         dma((4,)),
         dma((len(parts),)),
         dma((len(parts),)),
+        dma,
         dma,
         dma,
     ]

time: 87.8 us -> 85.8 us (0.977)
  Pallas kernels: 86.9 us -> 84.9 us
    pallas_call x1, Pallas kernels: 86.1 us -> 84 us  [on_device(): pl.pallas_call(functools.partial(layer_kernel, order, cap, parts, cuts),...]
where the time goes in v3:
time: 85.8 us; the launch traced here: 85.7 us
  Pallas kernels  84.9 us (99%)
    pallas_call x1, Pallas kernels, on_device(): pl.pallas_call(functools.partial(layer_kernel, order, cap, parts, cuts),...  84 us

profile of v3, /device:TPU:0, one launch (start us, length us, event | category | flops | bytes accessed | tf_op | source)
XLA Modules:
  0.0 85.7 jit_solution(7073170948165367883)
XLA Ops:
  0.6 84.0 %layer.1 = (bf16[128,1024]{1,0:T(8,128)(2,1)S(1)}, bf16[128,1024]{1,0:T(8,128)(2,1)S(1)}, f32[1,128]{1,0:T(1,128)S(1)}) custom-call(bf16[128,4096]{1,0:T(8,128)(2,1)} %tok_hbm.1, f32[1,4096]{1,0:T(1,128)} %bitcast.14, bf16[4,4096]{1,0:T(4,128)(2,1)} %bitcast.13, s32[2,128]{1,0:T(2,128)} %bitcast.16, bf16[4096,1024]{1,0:T(8,128)(2,1)} %bitcast.9, ...), custom_call_target="tpu_custom_call" | custom-call | tf_op jit(solution)/shard_map/layer/pallas_call | solution.py:905
  84.7 0.8 result.1
